TPU v7x, 512 devices: a whole 4x8x8 slice. The times are simulated.
512 devices in a mesh: gx: 128 (over z, y, core), gy: 4 (over x).
Axes of the slice: x: 4, y: 8, z: 8, core: 2. Of those that a mesh axis runs over, the one named last changes fastest.
Arguments:
- anomalies: float32 [80, 256, 32, 128], P(None, 'gx', 'gy'), may hold values from -6 to 6
- state_mean: float32 [256, 32, 128], P('gx', 'gy'), may hold values from -6 to 6
- obs_value: float32 [16, 256], P(None, 'gy'), may hold values from -8 to 8
- obs_cell: int32 [16, 256], replicated, may hold values from 0 to 2047
- owner: int32 [16], replicated, may hold values from 0 to 127, as said below
- order: int32 [16], replicated, may hold values from 0 to 15, each once
- root_inv: float32 [16, 256, 256], P(None, 'gy'), as said below
- gain_inv: float32 [16, 256, 256], P(None, 'gy'), as said below
Outputs:
- post_anomalies: float32 [80, 256, 32, 128], P(None, 'gx', 'gy')
- post_mean: float32 [256, 32, 128], P('gx', 'gy')
Inputs may be any that keep to these rules, and one draw needn't show every extreme that they name: `owner`: some batch lies at slab 128 - 2, some at slab 1 and some at slab 128 // 2; the others favour low slabs. `order`: each batch number once. `root_inv`: symmetric. `gain_inv`: symmetric.
All inputs are finite; a program needn't handle non-finite values.
Results may differ from a plain program's by a relative error of at most 0.0001.
Values sent between devices are 32-bit elements; how exact they have to be, the bound alone decides.
A program may use at most 64 MiB of HBM per device.

v0:
```python
import jax
import jax.numpy as jnp
from jax import lax
from jax.sharding import PartitionSpec as P

BATCHES = 16
REACH = 3


def shifted(value, axis, steps):
    count = lax.axis_size(axis)
    pairs = [(source, (source + steps) % count) for source in range(count)]
    return lax.ppermute(value, axis, pairs)


def gather_turned(arrays, axis, dims):
    turned = [jnp.moveaxis(a, dim, 0) for a, dim in zip(arrays, dims)]
    both = jnp.concatenate([t.reshape(len(t), -1) for t in turned], axis=1)
    out, at, done = (lax.all_gather(both, axis, axis=0, tiled=True), 0, [])
    for t, dim in zip(turned, dims):
        slab = out[:, at : at + t[0].size].reshape(-1, *t.shape[1:])
        done.append(jnp.moveaxis(slab, 0, dim))
        at += t[0].size
    return tuple(done)


def product(left_side, right_side):
    return jnp.dot(
        left_side, right_side, precision=lax.Precision.HIGHEST, preferred_element_type=jnp.float32
    )


def prior_relay(masked):
    total = masked
    upward = masked
    downward = masked
    for step in range(REACH):
        upward = shifted(upward, "gx", 1)
        downward = shifted(downward, "gx", -1)
        total = total + upward + downward
    return total


def local(anomalies, state_mean, obs_value, obs_cell, owner, order, root_inv, gain_inv):
    members, lon_dev, lat_dev, levels = anomalies.shape
    cell_count = lon_dev * lat_dev * levels
    quarter = obs_value.shape[1]
    obs_total = obs_cell.shape[1]
    slab_count = lax.axis_size("gx")
    band_count = lax.axis_size("gy")
    column = lax.axis_index("gx")
    band_index = lax.axis_index("gy")
    lon_total = slab_count * lon_dev
    lat_total = band_count * lat_dev
    taper_span = REACH * lon_dev + 1.0
    cell_ids = jnp.arange(cell_count, dtype=jnp.int32)
    cell_lon = column * lon_dev + cell_ids // (lat_dev * levels)
    cell_lat = band_index * lat_dev + cell_ids // levels % lat_dev
    obs_band = jnp.arange(obs_total, dtype=jnp.int32) // quarter

    def assimilate(batch_turn, carried):
        state_rows, mean_row = carried
        batch_id = order[batch_turn]
        root_slab = owner[batch_id]
        is_root = column == root_slab
        cells_of = obs_cell[batch_id]
        local_ids = lax.dynamic_slice_in_dim(cells_of, band_index * quarter, quarter)
        picked = jnp.take(state_rows, local_ids, axis=1)
        innovation = obs_value[batch_id] - jnp.take(mean_row, local_ids)
        root_rows = root_inv[batch_id]
        gain_rows = gain_inv[batch_id]
        joined = jnp.concatenate([picked, innovation[None, :]], axis=0)
        masked = jnp.where(is_root, joined, jnp.zeros_like(joined))
        joined = prior_relay(masked)
        picked, innovation = (joined[:members], joined[members])
        prior_all, innov_all = gather_turned((picked, innovation), "gy", (1, 0))
        weighted = product(prior_all, root_rows.T)
        gain_part = product(gain_rows, innov_all)
        weighted_all, gain_all = gather_turned((weighted, gain_part), "gy", (1, 0))
        obs_lon = root_slab * lon_dev + cells_of // (lat_dev * levels)
        obs_lat = obs_band * lat_dev + cells_of // levels % lat_dev
        slab_gap = jnp.abs(column - root_slab)
        in_reach = jnp.minimum(slab_gap, slab_count - slab_gap) <= REACH

        def near_update(operands):
            rows_now, mean_now = operands
            lon_gap = jnp.abs(obs_lon[:, None] - cell_lon[None, :])
            cycle_gap = jnp.minimum(lon_gap, lon_total - lon_gap)
            lat_gap = jnp.abs(obs_lat[:, None] - cell_lat[None, :])
            taper_rows = jnp.maximum(0.0, 1.0 - cycle_gap.astype(jnp.float32) / taper_span) * (
                1.0 - lat_gap.astype(jnp.float32) / lat_total
            )
            covariance = product(prior_all.T, rows_now) / (members - 1.0)
            gained = taper_rows * covariance
            stacked = jnp.concatenate([weighted_all, gain_all[None, :]], axis=0)
            increment = product(stacked, gained)
            return (rows_now - increment[:members], mean_now + increment[members])

        def keep_all(operands):
            return operands

        return lax.cond(in_reach, near_update, keep_all, (state_rows, mean_row))

    start_rows = anomalies.reshape(members, cell_count)
    start_mean = state_mean.reshape(cell_count)
    final_rows, final_mean = lax.fori_loop(0, BATCHES, assimilate, (start_rows, start_mean))
    return (
        final_rows.reshape(members, lon_dev, lat_dev, levels),
        final_mean.reshape(lon_dev, lat_dev, levels),
    )


def solution(mesh):
    return jax.shard_map(
        local,
        mesh=mesh,
        in_specs=(
            P(None, "gx", "gy", None),
            P("gx", "gy", None),
            P(None, "gy"),
            P(),
            P(),
            P(),
            P(None, "gy", None),
            P(None, "gy", None),
        ),
        out_specs=(P(None, "gx", "gy", None), P("gx", "gy", None)),
        check_vma=False,
    )
```

profile of v0, /device:TPU:2, one launch (start us, length us, event | category | flops | bytes accessed | tf_op | source)
XLA Modules:
  0.0 1054.0 jit_solution(2086697936089289550)
XLA Ops:
  3.4 1049.5 %while.19 = (s32[]{:T(128)}, f32[80,2048]{1,0:T(8,128)S(1)}, f32[2048]{0:T(1024)S(1)}, s32[16]{0:T(128)}, s32[16]{0:T(128)}, /*index=5*/s32[]{:T(128)}, s32[16,2...) while((s32[]{:T(128)}, f32[80,2048]{1,0:T(8,128)S(1)}, ...), condition=%wide.region_3.4_spmd.clone, body=%wide.region_0.3_spmd.clone.sunk | while | flops 1037565760 | bytes 11027220 | solution.py:106
  13.8 13.3 %collective-permute-start = (f32[81,64]{0,1:T(8,128)S(1)}, f32[81,64]{0,1:T(8,128)S(1)}, u32[]{:S(2)}, u32[]{:S(2)}) collective-permute-start(f32[81,64]{0,1:T(8,128)S(1)} %maximum_select_fusion.2), channel_id=1, source_target_pairs={{0,508},{4,0},{8,4},{12,8},{16,12},{20,16},{24,20},{28,24},{32,28}... | collective-permute-start | bytes 62216 | tf_op jit(solution)/shard_map/while/body/eval_jaxpr/ppermute | solution.py:13
  29.1 7.0 collective-permute-start.1
  38.0 7.0 collective-permute-start.2
  46.8 12.0 %all_gather.26 = f32[256,81]{1,0:T(8,128)S(1)} all-gather(f32[64,81]{1,0:T(8,128)S(1)} %pad_maximum_fusion.4), channel_id=1, replica_groups=mesh['gx'=128,'gy'=4] {'gy'}, dimensions={0}, use_global_device_ids=true | all-gather | bytes 103680 | tf_op jit(solution)/shard_map/while/body/eval_jaxpr/all_gather | solution.py:19
  61.2 12.0 %all_gather.27 = f32[256,81]{1,0:T(8,128)S(1)} all-gather(f32[64,81]{1,0:T(8,128)S(1)} %pad_maximum_fusion.5), channel_id=1, replica_groups=mesh['gx'=128,'gy'=4] {'gy'}, dimensions={0}, use_global_device_ids=true | all-gather | bytes 103680 | tf_op jit(solution)/shard_map/while/body/eval_jaxpr/all_gather | solution.py:19
  83.7 7.0 collective-permute-start
  92.6 7.0 collective-permute-start.1
  101.5 7.0 collective-permute-start.2
  110.3 12.0 %all_gather.26 = f32[256,81]{1,0:T(8,128)S(1)} all-gather(f32[64,81]{1,0:T(8,128)S(1)} %pad_maximum_fusion.4), channel_id=1, replica_groups=mesh['gx'=128,'gy'=4] {'gy'}, dimensions={0}, use_global_device_ids=true | all-gather | bytes 103680 | tf_op jit(solution)/shard_map/while/body/eval_jaxpr/all_gather | solution.py:19
  124.7 12.0 %all_gather.27 = f32[256,81]{1,0:T(8,128)S(1)} all-gather(f32[64,81]{1,0:T(8,128)S(1)} %pad_maximum_fusion.5), channel_id=1, replica_groups=mesh['gx'=128,'gy'=4] {'gy'}, dimensions={0}, use_global_device_ids=true | all-gather | bytes 103680 | tf_op jit(solution)/shard_map/while/body/eval_jaxpr/all_gather | solution.py:19
  152.7 7.0 collective-permute-start
  161.6 7.0 collective-permute-start.1
  170.5 7.0 collective-permute-start.2
  179.3 12.0 %all_gather.26 = f32[256,81]{1,0:T(8,128)S(1)} all-gather(f32[64,81]{1,0:T(8,128)S(1)} %pad_maximum_fusion.4), channel_id=1, replica_groups=mesh['gx'=128,'gy'=4] {'gy'}, dimensions={0}, use_global_device_ids=true | all-gather | bytes 103680 | tf_op jit(solution)/shard_map/while/body/eval_jaxpr/all_gather | solution.py:19
  193.7 12.0 %all_gather.27 = f32[256,81]{1,0:T(8,128)S(1)} all-gather(f32[64,81]{1,0:T(8,128)S(1)} %pad_maximum_fusion.5), channel_id=1, replica_groups=mesh['gx'=128,'gy'=4] {'gy'}, dimensions={0}, use_global_device_ids=true | all-gather | bytes 103680 | tf_op jit(solution)/shard_map/while/body/eval_jaxpr/all_gather | solution.py:19
  216.1 7.0 collective-permute-start
  225.1 7.0 collective-permute-start.1
  234.0 7.0 collective-permute-start.2
  242.8 12.0 %all_gather.26 = f32[256,81]{1,0:T(8,128)S(1)} all-gather(f32[64,81]{1,0:T(8,128)S(1)} %pad_maximum_fusion.4), channel_id=1, replica_groups=mesh['gx'=128,'gy'=4] {'gy'}, dimensions={0}, use_global_device_ids=true | all-gather | bytes 103680 | tf_op jit(solution)/shard_map/while/body/eval_jaxpr/all_gather | solution.py:19
  257.1 12.0 %all_gather.27 = f32[256,81]{1,0:T(8,128)S(1)} all-gather(f32[64,81]{1,0:T(8,128)S(1)} %pad_maximum_fusion.5), channel_id=1, replica_groups=mesh['gx'=128,'gy'=4] {'gy'}, dimensions={0}, use_global_device_ids=true | all-gather | bytes 103680 | tf_op jit(solution)/shard_map/while/body/eval_jaxpr/all_gather | solution.py:19
  285.2 7.0 collective-permute-start
  294.1 7.0 collective-permute-start.1
  303.0 7.0 collective-permute-start.2
  311.8 12.0 %all_gather.26 = f32[256,81]{1,0:T(8,128)S(1)} all-gather(f32[64,81]{1,0:T(8,128)S(1)} %pad_maximum_fusion.4), channel_id=1, replica_groups=mesh['gx'=128,'gy'=4] {'gy'}, dimensions={0}, use_global_device_ids=true | all-gather | bytes 103680 | tf_op jit(solution)/shard_map/while/body/eval_jaxpr/all_gather | solution.py:19
  326.2 12.0 %all_gather.27 = f32[256,81]{1,0:T(8,128)S(1)} all-gather(f32[64,81]{1,0:T(8,128)S(1)} %pad_maximum_fusion.5), channel_id=1, replica_groups=mesh['gx'=128,'gy'=4] {'gy'}, dimensions={0}, use_global_device_ids=true | all-gather | bytes 103680 | tf_op jit(solution)/shard_map/while/body/eval_jaxpr/all_gather | solution.py:19
  348.6 7.0 collective-permute-start
  357.5 7.0 collective-permute-start.1
  366.5 7.0 collective-permute-start.2
  375.3 12.0 %all_gather.26 = f32[256,81]{1,0:T(8,128)S(1)} all-gather(f32[64,81]{1,0:T(8,128)S(1)} %pad_maximum_fusion.4), channel_id=1, replica_groups=mesh['gx'=128,'gy'=4] {'gy'}, dimensions={0}, use_global_device_ids=true | all-gather | bytes 103680 | tf_op jit(solution)/shard_map/while/body/eval_jaxpr/all_gather | solution.py:19
  389.6 12.0 %all_gather.27 = f32[256,81]{1,0:T(8,128)S(1)} all-gather(f32[64,81]{1,0:T(8,128)S(1)} %pad_maximum_fusion.5), channel_id=1, replica_groups=mesh['gx'=128,'gy'=4] {'gy'}, dimensions={0}, use_global_device_ids=true | all-gather | bytes 103680 | tf_op jit(solution)/shard_map/while/body/eval_jaxpr/all_gather | solution.py:19
  417.6 7.0 collective-permute-start
  426.6 7.0 collective-permute-start.1
  435.5 7.0 collective-permute-start.2
  444.3 12.0 %all_gather.26 = f32[256,81]{1,0:T(8,128)S(1)} all-gather(f32[64,81]{1,0:T(8,128)S(1)} %pad_maximum_fusion.4), channel_id=1, replica_groups=mesh['gx'=128,'gy'=4] {'gy'}, dimensions={0}, use_global_device_ids=true | all-gather | bytes 103680 | tf_op jit(solution)/shard_map/while/body/eval_jaxpr/all_gather | solution.py:19
  458.6 12.0 %all_gather.27 = f32[256,81]{1,0:T(8,128)S(1)} all-gather(f32[64,81]{1,0:T(8,128)S(1)} %pad_maximum_fusion.5), channel_id=1, replica_groups=mesh['gx'=128,'gy'=4] {'gy'}, dimensions={0}, use_global_device_ids=true | all-gather | bytes 103680 | tf_op jit(solution)/shard_map/while/body/eval_jaxpr/all_gather | solution.py:19
  481.1 7.0 collective-permute-start
  490.0 7.0 collective-permute-start.1
  498.9 7.0 collective-permute-start.2
  507.8 12.0 %all_gather.26 = f32[256,81]{1,0:T(8,128)S(1)} all-gather(f32[64,81]{1,0:T(8,128)S(1)} %pad_maximum_fusion.4), channel_id=1, replica_groups=mesh['gx'=128,'gy'=4] {'gy'}, dimensions={0}, use_global_device_ids=true | all-gather | bytes 103680 | tf_op jit(solution)/shard_map/while/body/eval_jaxpr/all_gather | solution.py:19
  522.1 12.0 %all_gather.27 = f32[256,81]{1,0:T(8,128)S(1)} all-gather(f32[64,81]{1,0:T(8,128)S(1)} %pad_maximum_fusion.5), channel_id=1, replica_groups=mesh['gx'=128,'gy'=4] {'gy'}, dimensions={0}, use_global_device_ids=true | all-gather | bytes 103680 | tf_op jit(solution)/shard_map/while/body/eval_jaxpr/all_gather | solution.py:19
  544.5 7.0 collective-permute-start
  553.5 7.0 collective-permute-start.1
  571.2 12.0 %all_gather.26 = f32[256,81]{1,0:T(8,128)S(1)} all-gather(f32[64,81]{1,0:T(8,128)S(1)} %pad_maximum_fusion.4), channel_id=1, replica_groups=mesh['gx'=128,'gy'=4] {'gy'}, dimensions={0}, use_global_device_ids=true | all-gather | bytes 103680 | tf_op jit(solution)/shard_map/while/body/eval_jaxpr/all_gather | solution.py:19
  585.6 12.0 %all_gather.27 = f32[256,81]{1,0:T(8,128)S(1)} all-gather(f32[64,81]{1,0:T(8,128)S(1)} %pad_maximum_fusion.5), channel_id=1, replica_groups=mesh['gx'=128,'gy'=4] {'gy'}, dimensions={0}, use_global_device_ids=true | all-gather | bytes 103680 | tf_op jit(solution)/shard_map/while/body/eval_jaxpr/all_gather | solution.py:19
  608.0 7.0 collective-permute-start
  625.9 7.0 collective-permute-start.2
  634.7 12.0 %all_gather.26 = f32[256,81]{1,0:T(8,128)S(1)} all-gather(f32[64,81]{1,0:T(8,128)S(1)} %pad_maximum_fusion.4), channel_id=1, replica_groups=mesh['gx'=128,'gy'=4] {'gy'}, dimensions={0}, use_global_device_ids=true | all-gather | bytes 103680 | tf_op jit(solution)/shard_map/while/body/eval_jaxpr/all_gather | solution.py:19
  649.0 12.0 %all_gather.27 = f32[256,81]{1,0:T(8,128)S(1)} all-gather(f32[64,81]{1,0:T(8,128)S(1)} %pad_maximum_fusion.5), channel_id=1, replica_groups=mesh['gx'=128,'gy'=4] {'gy'}, dimensions={0}, use_global_device_ids=true | all-gather | bytes 103680 | tf_op jit(solution)/shard_map/while/body/eval_jaxpr/all_gather | solution.py:19
  698.1 12.0 %all_gather.26 = f32[256,81]{1,0:T(8,128)S(1)} all-gather(f32[64,81]{1,0:T(8,128)S(1)} %pad_maximum_fusion.4), channel_id=1, replica_groups=mesh['gx'=128,'gy'=4] {'gy'}, dimensions={0}, use_global_device_ids=true | all-gather | bytes 103680 | tf_op jit(solution)/shard_map/while/body/eval_jaxpr/all_gather | solution.py:19
  712.5 12.0 %all_gather.27 = f32[256,81]{1,0:T(8,128)S(1)} all-gather(f32[64,81]{1,0:T(8,128)S(1)} %pad_maximum_fusion.5), channel_id=1, replica_groups=mesh['gx'=128,'gy'=4] {'gy'}, dimensions={0}, use_global_device_ids=true | all-gather | bytes 103680 | tf_op jit(solution)/shard_map/while/body/eval_jaxpr/all_gather | solution.py:19
  761.6 12.0 %all_gather.26 = f32[256,81]{1,0:T(8,128)S(1)} all-gather(f32[64,81]{1,0:T(8,128)S(1)} %pad_maximum_fusion.4), channel_id=1, replica_groups=mesh['gx'=128,'gy'=4] {'gy'}, dimensions={0}, use_global_device_ids=true | all-gather | bytes 103680 | tf_op jit(solution)/shard_map/while/body/eval_jaxpr/all_gather | solution.py:19
  775.9 12.0 %all_gather.27 = f32[256,81]{1,0:T(8,128)S(1)} all-gather(f32[64,81]{1,0:T(8,128)S(1)} %pad_maximum_fusion.5), channel_id=1, replica_groups=mesh['gx'=128,'gy'=4] {'gy'}, dimensions={0}, use_global_device_ids=true | all-gather | bytes 103680 | tf_op jit(solution)/shard_map/while/body/eval_jaxpr/all_gather | solution.py:19
  825.1 12.0 %all_gather.26 = f32[256,81]{1,0:T(8,128)S(1)} all-gather(f32[64,81]{1,0:T(8,128)S(1)} %pad_maximum_fusion.4), channel_id=1, replica_groups=mesh['gx'=128,'gy'=4] {'gy'}, dimensions={0}, use_global_device_ids=true | all-gather | bytes 103680 | tf_op jit(solution)/shard_map/while/body/eval_jaxpr/all_gather | solution.py:19
  839.4 12.0 %all_gather.27 = f32[256,81]{1,0:T(8,128)S(1)} all-gather(f32[64,81]{1,0:T(8,128)S(1)} %pad_maximum_fusion.5), channel_id=1, replica_groups=mesh['gx'=128,'gy'=4] {'gy'}, dimensions={0}, use_global_device_ids=true | all-gather | bytes 103680 | tf_op jit(solution)/shard_map/while/body/eval_jaxpr/all_gather | solution.py:19
  876.3 7.0 collective-permute-start.1
  894.1 12.0 %all_gather.26 = f32[256,81]{1,0:T(8,128)S(1)} all-gather(f32[64,81]{1,0:T(8,128)S(1)} %pad_maximum_fusion.4), channel_id=1, replica_groups=mesh['gx'=128,'gy'=4] {'gy'}, dimensions={0}, use_global_device_ids=true | all-gather | bytes 103680 | tf_op jit(solution)/shard_map/while/body/eval_jaxpr/all_gather | solution.py:19
  908.4 12.0 %all_gather.27 = f32[256,81]{1,0:T(8,128)S(1)} all-gather(f32[64,81]{1,0:T(8,128)S(1)} %pad_maximum_fusion.5), channel_id=1, replica_groups=mesh['gx'=128,'gy'=4] {'gy'}, dimensions={0}, use_global_device_ids=true | all-gather | bytes 103680 | tf_op jit(solution)/shard_map/while/body/eval_jaxpr/all_gather | solution.py:19
  957.5 12.0 %all_gather.26 = f32[256,81]{1,0:T(8,128)S(1)} all-gather(f32[64,81]{1,0:T(8,128)S(1)} %pad_maximum_fusion.4), channel_id=1, replica_groups=mesh['gx'=128,'gy'=4] {'gy'}, dimensions={0}, use_global_device_ids=true | all-gather | bytes 103680 | tf_op jit(solution)/shard_map/while/body/eval_jaxpr/all_gather | solution.py:19
  971.9 12.0 %all_gather.27 = f32[256,81]{1,0:T(8,128)S(1)} all-gather(f32[64,81]{1,0:T(8,128)S(1)} %pad_maximum_fusion.5), channel_id=1, replica_groups=mesh['gx'=128,'gy'=4] {'gy'}, dimensions={0}, use_global_device_ids=true | all-gather | bytes 103680 | tf_op jit(solution)/shard_map/while/body/eval_jaxpr/all_gather | solution.py:19
  994.3 7.0 collective-permute-start
  1012.2 7.0 collective-permute-start.2
  1021.0 12.0 %all_gather.26 = f32[256,81]{1,0:T(8,128)S(1)} all-gather(f32[64,81]{1,0:T(8,128)S(1)} %pad_maximum_fusion.4), channel_id=1, replica_groups=mesh['gx'=128,'gy'=4] {'gy'}, dimensions={0}, use_global_device_ids=true | all-gather | bytes 103680 | tf_op jit(solution)/shard_map/while/body/eval_jaxpr/all_gather | solution.py:19
  1035.3 12.0 %all_gather.27 = f32[256,81]{1,0:T(8,128)S(1)} all-gather(f32[64,81]{1,0:T(8,128)S(1)} %pad_maximum_fusion.5), channel_id=1, replica_groups=mesh['gx'=128,'gy'=4] {'gy'}, dimensions={0}, use_global_device_ids=true | all-gather | bytes 103680 | tf_op jit(solution)/shard_map/while/body/eval_jaxpr/all_gather | solution.py:19
  (761 shorter events, 413.0 us)
Async XLA Ops:
  11.9 15.2 %collective-permute-start.3 = (f32[81,64]{0,1:T(8,128)S(1)}, f32[81,64]{0,1:T(8,128)S(1)}, u32[]{:S(2)}, u32[]{:S(2)}) collective-permute-start(f32[81,64]{0,1:T(8,128)S(1)} %maximum_select_fusion.2), channel_id=1, source_target_pairs={{0,4},{4,8},{8,12},{12,16},{16,20},{20,24},{24,28},{28,32},{32,36}... | collective-permute-start | bytes 62216 | tf_op jit(solution)/shard_map/while/body/eval_jaxpr/ppermute | solution.py:13
  13.8 15.3 %collective-permute-start = (f32[81,64]{0,1:T(8,128)S(1)}, f32[81,64]{0,1:T(8,128)S(1)}, u32[]{:S(2)}, u32[]{:S(2)}) collective-permute-start(f32[81,64]{0,1:T(8,128)S(1)} %maximum_select_fusion.2), channel_id=1, source_target_pairs={{0,508},{4,0},{8,4},{12,8},{16,12},{20,16},{24,20},{28,24},{32,28}... | collective-permute-start | bytes 62216 | tf_op jit(solution)/shard_map/while/body/eval_jaxpr/ppermute | solution.py:13
  27.1 8.9 collective-permute-start.4
  29.1 8.9 collective-permute-start.1
  36.1 9.8 collective-permute-start.5
  83.7 8.9 collective-permute-start
  90.7 8.9 collective-permute-start.4
  92.6 8.9 collective-permute-start.1
  99.6 9.8 collective-permute-start.5
  152.7 8.9 collective-permute-start
  159.7 8.9 collective-permute-start.4
  161.6 8.9 collective-permute-start.1
  168.6 9.8 collective-permute-start.5
  216.1 8.9 collective-permute-start
  223.1 8.9 collective-permute-start.4
  225.1 8.9 collective-permute-start.1
  232.1 9.8 collective-permute-start.5
  285.2 8.9 collective-permute-start
  292.1 8.9 collective-permute-start.4
  294.1 8.9 collective-permute-start.1
  301.1 9.8 collective-permute-start.5
  348.6 8.9 collective-permute-start
  355.6 8.9 collective-permute-start.4
  357.5 8.9 collective-permute-start.1
  364.5 9.8 collective-permute-start.5
  417.6 8.9 collective-permute-start
  424.6 8.9 collective-permute-start.4
  426.6 8.9 collective-permute-start.1
  433.6 9.8 collective-permute-start.5
  481.1 8.9 collective-permute-start
  488.1 8.9 collective-permute-start.4
  490.0 8.9 collective-permute-start.1
  497.0 9.8 collective-permute-start.5
  544.5 8.9 collective-permute-start
  551.5 8.9 collective-permute-start.4
  553.5 8.9 collective-permute-start.1
  560.5 9.8 collective-permute-start.5
  608.0 8.9 collective-permute-start
  615.0 8.9 collective-permute-start.4
  616.9 8.9 collective-permute-start.1
  623.9 9.8 collective-permute-start.5
  671.5 8.9 collective-permute-start
  678.5 8.9 collective-permute-start.4
  680.4 8.9 collective-permute-start.1
  687.4 9.8 collective-permute-start.5
  734.9 8.9 collective-permute-start
  741.9 8.9 collective-permute-start.4
  743.9 8.9 collective-permute-start.1
  750.9 9.8 collective-permute-start.5
  798.4 8.9 collective-permute-start
  805.4 8.9 collective-permute-start.4
  807.3 8.9 collective-permute-start.1
  814.3 9.8 collective-permute-start.5
  867.4 8.9 collective-permute-start
  874.4 8.9 collective-permute-start.4
  876.3 8.9 collective-permute-start.1
  883.3 9.8 collective-permute-start.5
  930.9 8.9 collective-permute-start
  937.9 8.9 collective-permute-start.4
  939.8 8.9 collective-permute-start.1
  946.8 9.8 collective-permute-start.5
  1001.3 8.9 collective-permute-start.4
  1003.3 8.9 collective-permute-start.1
  1010.3 9.8 collective-permute-start.5
  (33 other events, 280.3 us)
where the time goes:
time: 1060 us; the launch traced here: 1050 us
  starting transfers between devices  433 us (41%)
  blocking collectives  384 us (36%)
  local copies, waits for them, and re-layouts  98.4 us (9%)
  loops' own time  62.6 us (6%)
  matrix products  55.5 us (5%)
  waiting for transfers between devices  11.1 us (1%)
    ppermute x96, starting transfers between devices, shifted(): return lax.ppermute(value, axis, pairs)  433 us
    all_gather x32, blocking collectives, gather_turned(): out, at, done = (lax.all_gather(both, axis, axis=0, tiled=True), 0, [])  384 us
    another operation x1, loops' own time, local(): lax.fori_loop(0, BATCHES, assimilate, (start_rows, start_mean))  58.7 us
    dot_general x42, matrix products, product(): jnp.dot(left_side, right_side, precision=lax.Precision.HIGHEST, preferred...  55.5 us
  transfers between devices with their start and end apart: 96, of which 16 were waited for; matrix products, arithmetic and copies ran while one was open for 0% of the time, Pallas kernels for 0%

commit v1 on v0

--- a/solution.py
+++ b/solution.py
@@ -16,7 +16,13 @@
 def gather_turned(arrays, axis, dims):
     turned = [jnp.moveaxis(a, dim, 0) for a, dim in zip(arrays, dims)]
     both = jnp.concatenate([t.reshape(len(t), -1) for t in turned], axis=1)
-    out, at, done = (lax.all_gather(both, axis, axis=0, tiled=True), 0, [])
+    out, at, done = (
+        jnp.concatenate(
+            lax.all_to_all(jnp.stack([both] * lax.axis_size(axis)), axis, 0, 0), axis=0
+        ),
+        0,
+        [],
+    )
     for t, dim in zip(turned, dims):
         slab = out[:, at : at + t[0].size].reshape(-1, *t.shape[1:])
         done.append(jnp.moveaxis(slab, 0, dim))

time: 1060 us -> 991 us (0.935)
  blocking collectives: 384 us -> 0 us
  starting transfers between devices: 433 us -> 585 us
  waiting for transfers between devices: 11.1 us -> 158 us
  local copies, waits for them, and re-layouts: 98.4 us -> 118 us
    all_gather x32 -> x0, blocking collectives: 384 us -> none  [gather_turned(): out, at, done = (lax.all_gather(both, axis, axis=0, tiled=True), 0, [])]
    all_to_all x0 -> x32, starting transfers between devices: none -> 152 us  [gather_turned(): lax.all_to_all(jnp.stack([both] * lax.axis_size(axis)), axis, 0, 0)]
    all_to_all x0 -> x32, waiting for transfers between devices: none -> 145 us  [gather_turned(): lax.all_to_all(jnp.stack([both] * lax.axis_size(axis)), axis, 0, 0)]
    another operation x26 -> x58, local copies, waits for them, and re-layouts: 0.96 us -> 22.5 us  [the longest x32 21.5 us: gather_turned(): jnp.stack([both] * lax.axis_size(axis))]
  transfers between devices with their start and end apart: 96 -> 128, of which waited for: 16 -> 48; matrix products, arithmetic and copies ran while one was open for 0% -> 0% of each run, Pallas kernels for 0% -> 0%
where the time goes in v1:
time: 991 us; the launch traced here: 982 us
  starting transfers between devices  585 us (59%)
  waiting for transfers between devices  158 us (16%)
  local copies, waits for them, and re-layouts  118 us (12%)
  loops' own time  56.3 us (6%)
  matrix products  55.5 us (6%)
    ppermute x96, starting transfers between devices, shifted(): return lax.ppermute(value, axis, pairs)  433 us
    all_to_all x32, starting transfers between devices, gather_turned(): lax.all_to_all(jnp.stack([both] * lax.axis_size(axis)), axis, 0, 0)  152 us
    all_to_all x32, waiting for transfers between devices, gather_turned(): lax.all_to_all(jnp.stack([both] * lax.axis_size(axis)), axis, 0, 0)  145 us
    dot_general x42, matrix products, product(): jnp.dot(left_side, right_side, precision=lax.Precision.HIGHEST, preferred...  55.5 us
    another operation x1, loops' own time, local(): lax.fori_loop(0, BATCHES, assimilate, (start_rows, start_mean))  53 us
    another operation x32, local copies, waits for them, and re-layouts, gather_turned(): jnp.stack([both] * lax.axis_size(axis))  21.5 us
    dynamic_slice x16, local copies, waits for them, and re-layouts, assimilate(): root_slab = owner[batch_id]  19.9 us
    dynamic_slice x16, local copies, waits for them, and re-layouts, assimilate(): batch_id = order[batch_turn]  19.9 us
  transfers between devices with their start and end apart: 128, of which 48 were waited for; matrix products, arithmetic and copies ran while one was open for 0% of the time, Pallas kernels for 0%

profile of v1, /device:TPU:2, one launch (start us, length us, event | category | flops | bytes accessed | tf_op | source)
XLA Modules:
  0.0 982.0 jit_solution(991513052951710378)
XLA Ops:
  3.4 977.6 %while.19 = (s32[]{:T(128)}, f32[80,2048]{1,0:T(8,128)S(1)}, f32[2048]{0:T(1024)S(1)}, s32[16]{0:T(128)}, s32[16]{0:T(128)}, /*index=5*/s32[]{:T(128)}, s32[16,2...) while((s32[]{:T(128)}, f32[80,2048]{1,0:T(8,128)S(1)}, ...), condition=%wide.region_3.4_spmd.clone, body=%wide.region_0.3_spmd.clone.sunk | while | flops 1037565760 | bytes 11717460 | solution.py:112
  13.5 13.3 %collective-permute-start = (f32[81,64]{0,1:T(8,128)S(1)}, f32[81,64]{0,1:T(8,128)S(1)}, u32[]{:S(2)}, u32[]{:S(2)}) collective-permute-start(f32[81,64]{0,1:T(8,128)S(1)} %maximum_select_fusion.2), channel_id=1, source_target_pairs={{0,508},{4,0},{8,4},{12,8},{16,12},{20,16},{24,20},{28,24},{32,28}... | collective-permute-start | bytes 62216 | tf_op jit(solution)/shard_map/while/body/eval_jaxpr/ppermute | solution.py:13
  28.7 7.0 collective-permute-start.1
  37.6 7.0 collective-permute-start.2
  47.1 4.8 all-to-all-start
  59.5 4.8 all-to-all-start.1
  78.9 7.0 collective-permute-start
  87.8 7.0 collective-permute-start.1
  96.7 7.0 collective-permute-start.2
  127.8 5.5 conditional.3
  143.3 7.0 collective-permute-start
  152.2 7.0 collective-permute-start.1
  161.1 7.0 collective-permute-start.2
  182.9 4.8 all-to-all-start.1
  202.3 7.0 collective-permute-start
  211.2 7.0 collective-permute-start.1
  220.1 7.0 collective-permute-start.2
  251.2 5.4 conditional.3
  266.7 7.0 collective-permute-start
  275.6 7.0 collective-permute-start.1
  284.6 7.0 collective-permute-start.2
  294.0 4.8 all-to-all-start
  325.7 7.0 collective-permute-start
  334.6 7.0 collective-permute-start.1
  343.6 7.0 collective-permute-start.2
  374.7 5.5 conditional.3
  390.2 7.0 collective-permute-start
  399.1 7.0 collective-permute-start.1
  408.0 7.0 collective-permute-start.2
  449.1 7.0 collective-permute-start
  458.1 7.0 collective-permute-start.1
  467.0 7.0 collective-permute-start.2
  488.8 4.8 all-to-all-start.1
  508.1 7.0 collective-permute-start
  517.1 7.0 collective-permute-start.1
  526.0 7.0 collective-permute-start.2
  547.8 4.8 all-to-all-start.1
  567.1 7.0 collective-permute-start
  576.1 7.0 collective-permute-start.1
  585.0 7.0 collective-permute-start.2
  606.8 4.8 all-to-all-start.1
  626.1 7.0 collective-permute-start
  635.1 7.0 collective-permute-start.1
  644.0 7.0 collective-permute-start.2
  665.8 4.8 all-to-all-start.1
  685.1 7.0 collective-permute-start
  694.1 7.0 collective-permute-start.1
  703.0 7.0 collective-permute-start.2
  724.8 4.8 all-to-all-start.1
  744.1 7.0 collective-permute-start
  753.1 7.0 collective-permute-start.1
  762.0 7.0 collective-permute-start.2
  783.8 4.8 all-to-all-start.1
  793.1 5.5 conditional.3
  808.6 7.0 collective-permute-start
  817.5 7.0 collective-permute-start.1
  826.4 7.0 collective-permute-start.2
  867.6 7.0 collective-permute-start
  876.5 7.0 collective-permute-start.1
  885.4 7.0 collective-permute-start.2
  926.6 7.0 collective-permute-start
  935.5 7.0 collective-permute-start.1
  944.4 7.0 collective-permute-start.2
  975.5 5.5 conditional.3
  (825 shorter events, 537.1 us)
Async XLA Ops:
  11.5 15.2 %collective-permute-start.3 = (f32[81,64]{0,1:T(8,128)S(1)}, f32[81,64]{0,1:T(8,128)S(1)}, u32[]{:S(2)}, u32[]{:S(2)}) collective-permute-start(f32[81,64]{0,1:T(8,128)S(1)} %maximum_select_fusion.2), channel_id=1, source_target_pairs={{0,4},{4,8},{8,12},{12,16},{16,20},{20,24},{24,28},{28,32},{32,36}... | collective-permute-start | bytes 62216 | tf_op jit(solution)/shard_map/while/body/eval_jaxpr/ppermute | solution.py:13
  13.5 15.2 %collective-permute-start = (f32[81,64]{0,1:T(8,128)S(1)}, f32[81,64]{0,1:T(8,128)S(1)}, u32[]{:S(2)}, u32[]{:S(2)}) collective-permute-start(f32[81,64]{0,1:T(8,128)S(1)} %maximum_select_fusion.2), channel_id=1, source_target_pairs={{0,508},{4,0},{8,4},{12,8},{16,12},{20,16},{24,20},{28,24},{32,28}... | collective-permute-start | bytes 62216 | tf_op jit(solution)/shard_map/while/body/eval_jaxpr/ppermute | solution.py:13
  26.8 8.9 collective-permute-start.4
  28.7 8.9 collective-permute-start.1
  35.7 9.7 collective-permute-start.5
  47.1 9.3 all-to-all-start
  59.5 9.3 all-to-all-start.1
  78.9 8.9 collective-permute-start
  85.8 8.9 collective-permute-start.4
  87.8 8.9 collective-permute-start.1
  94.8 9.7 collective-permute-start.5
  106.2 9.3 all-to-all-start
  118.5 9.3 all-to-all-start.1
  143.3 8.9 collective-permute-start
  150.3 8.9 collective-permute-start.4
  152.2 8.9 collective-permute-start.1
  159.2 9.7 collective-permute-start.5
  170.6 9.3 all-to-all-start
  182.9 9.3 all-to-all-start.1
  209.3 8.9 collective-permute-start.4
  211.2 8.9 collective-permute-start.1
  218.2 9.7 collective-permute-start.5
  229.6 9.3 all-to-all-start
  241.9 9.3 all-to-all-start.1
  266.7 8.9 collective-permute-start
  273.7 8.9 collective-permute-start.4
  275.6 8.9 collective-permute-start.1
  282.6 9.7 collective-permute-start.5
  294.0 9.3 all-to-all-start
  306.3 9.3 all-to-all-start.1
  325.7 8.9 collective-permute-start
  341.6 9.7 collective-permute-start.5
  353.0 9.3 all-to-all-start
  365.3 9.3 all-to-all-start.1
  406.1 9.7 collective-permute-start.5
  417.5 9.3 all-to-all-start
  429.8 9.3 all-to-all-start.1
  465.0 9.7 collective-permute-start.5
  476.5 9.3 all-to-all-start
  488.8 9.3 all-to-all-start.1
  524.0 9.7 collective-permute-start.5
  535.5 9.3 all-to-all-start
  547.8 9.3 all-to-all-start.1
  583.0 9.7 collective-permute-start.5
  594.5 9.3 all-to-all-start
  606.8 9.3 all-to-all-start.1
  642.0 9.7 collective-permute-start.5
  653.5 9.3 all-to-all-start
  665.8 9.3 all-to-all-start.1
  701.0 9.7 collective-permute-start.5
  712.5 9.3 all-to-all-start
  724.8 9.3 all-to-all-start.1
  760.0 9.7 collective-permute-start.5
  771.5 9.3 all-to-all-start
  783.8 9.3 all-to-all-start.1
  824.5 9.7 collective-permute-start.5
  835.9 9.3 all-to-all-start
  848.2 9.3 all-to-all-start.1
  883.5 9.7 collective-permute-start.5
  894.9 9.3 all-to-all-start
  907.2 9.3 all-to-all-start.1
  942.5 9.7 collective-permute-start.5
  953.9 9.3 all-to-all-start
  966.2 9.3 all-to-all-start.1
  (65 other events, 565.3 us)
